TPU v7x, 32 devices: a whole 2x2x4 slice. The times are simulated.
32 devices in a mesh: obs: 8 (over z, y), chan: 4 (over x, core).
Axes of the slice: x: 2, y: 2, z: 4, core: 2. Of those that a mesh axis runs over, the one named last changes fastest.
Arguments:
- jacobian: bfloat16 [2048, 128, 137], P('obs', 'chan'), may hold values from -0.5 to 0.5
- departures: float32 [128, 2048], P('chan', 'obs'), may hold values from -6 to 6
- obs_weights: float32 [128, 2048], P('chan', 'obs'), may hold values from 0.25 to 4
- column_count: int32 [8], P('obs'), may hold values from 1 to 256, as said below
- grid_block: int32 [16], P('obs'), may hold values from 0 to 15, as said below
- sqrt_cov: float32 [137, 137], replicated, may hold values from -0.5 to 0.5
Outputs:
- increment: float32 [2048, 137], P('obs')
- residual: float32 [2048, 137], P('obs')
Inputs may be any that keep to these rules, and one draw needn't show every extreme that they name: The first column_count of a device's 256 column slots are observed; some device has all 256 observed in every draw. `grid_block`: the owner of grid block g is index g // 2 of obs. The 2 blocks of one device match blocks of 2 different owners; in every draw some owner has a block matched by each device (every device matches one of that owner's blocks), and some device matches that owner's last block.
All inputs are finite; a program needn't handle non-finite values.
Results may differ from a plain program's by a relative error of at most 0.02.
Values may be sent and summed in bfloat16 or wider, within the bound.
A program may use at most 64 MiB of HBM per device.

v0:
```python
import jax
import jax.numpy as jnp
from jax import lax
from jax.sharding import PartitionSpec as P

BLOCK = 128
ITERS = 5
GRID_BLK = 2


def block_terms(jac_part, weight_part, mask_part, predicted):
    scaled = (mask_part[:, None] * weight_part * predicted).astype(jnp.bfloat16)
    return lax.dot_general(
        jac_part, scaled, (((1,), (1,)), ((0,), (0,))), preferred_element_type=jnp.float32
    )


def forward_terms(jac_part, weight_part, mask_part, field_part):
    predicted = lax.dot_general(
        jac_part, field_part, (((2,), (1,)), ((0,), (0,))), preferred_element_type=jnp.float32
    )
    return block_terms(jac_part, weight_part, mask_part, predicted)


def per_device(jacobian, departures, obs_weights, column_count, grid_block, sqrt_cov):
    obs_count = lax.axis_size("obs")
    myself = lax.axis_index("obs")
    capacity, group_channels, layers = jacobian.shape
    block_count = capacity // BLOCK
    weight_cols = obs_weights.T
    depart_cols = departures.T
    observed = (jnp.arange(capacity, dtype=jnp.int32) < column_count[0]).astype(jnp.float32)
    every_id = lax.all_gather(grid_block, "obs", axis=0, tiled=True).reshape(obs_count, block_count)
    targets = jnp.arange(obs_count, dtype=jnp.int32)
    send_pick = (grid_block[None, :] // GRID_BLK == targets[:, None]).astype(jnp.float32)
    owned_here = every_id // GRID_BLK == myself
    places = every_id % GRID_BLK
    grid_index = jnp.arange(GRID_BLK, dtype=jnp.int32)
    take_pick = jnp.sum(
        ((places[None] == grid_index[:, None, None]) & owned_here[None]).astype(jnp.float32), axis=2
    )
    share_cols = BLOCK

    def local_terms(kernel_fn, inputs):
        return kernel_fn(jacobian, weight_cols, observed, inputs)

    def to_owners(terms):
        blocked = terms.reshape(block_count, BLOCK, layers)
        blocked = lax.psum(blocked, "chan")
        outgoing = jnp.dot(
            send_pick, blocked.reshape(block_count, -1), precision=lax.Precision.HIGHEST
        )
        incoming = lax.all_to_all(
            outgoing.reshape(obs_count, share_cols, layers),
            "obs",
            split_axis=0,
            concat_axis=0,
            tiled=True,
        )
        summed = jnp.dot(
            take_pick, incoming.reshape(obs_count, -1), precision=lax.Precision.HIGHEST
        )
        return summed.reshape(GRID_BLK, share_cols, layers)

    def spread(field):
        return jnp.dot(
            field.reshape(-1, layers), sqrt_cov, precision=lax.Precision.HIGHEST
        ).reshape(field.shape)

    def spread_back(field):
        flat = lax.dot_general(
            field.reshape(-1, layers),
            sqrt_cov,
            (((1,), (1,)), ((), ())),
            precision=lax.Precision.HIGHEST,
        )
        return flat.reshape(field.shape)

    def squared(values):
        partial_sum = jnp.sum(values * values)
        return lax.psum(partial_sum, "obs")

    residual = spread_back(to_owners(local_terms(block_terms, depart_cols)))
    control = jnp.zeros_like(residual)
    direction = residual
    norm_now = squared(residual)
    for iteration in range(ITERS):
        rounded = spread(direction).astype(jnp.bfloat16).reshape(GRID_BLK, -1)
        to_outgoing = jnp.dot(
            take_pick.T.astype(jnp.bfloat16), rounded, preferred_element_type=jnp.float32
        ).astype(jnp.bfloat16)
        to_incoming = lax.all_to_all(
            to_outgoing.reshape(obs_count, share_cols, layers),
            "obs",
            split_axis=0,
            concat_axis=0,
            tiled=True,
        )
        picked = jnp.dot(
            send_pick.T.astype(jnp.bfloat16),
            to_incoming.reshape(obs_count, -1),
            preferred_element_type=jnp.float32,
        )
        picked = picked.astype(jnp.bfloat16).reshape(block_count, share_cols, layers)
        fetched = picked.reshape(capacity, layers)
        image = direction + spread_back(to_owners(local_terms(forward_terms, fetched)))
        curvature_partial_sum = jnp.sum(direction * image)
        step_length = norm_now / lax.psum(curvature_partial_sum, "obs")
        control = control + step_length * direction
        residual = residual - step_length * image
        norm_next = squared(residual)
        direction = residual + norm_next / norm_now * direction
        norm_now = norm_next
    increment = spread(control)
    return (increment.reshape(-1, layers), residual.reshape(-1, layers))


def solution(mesh):
    in_specs = (P("obs", "chan", None), P("chan", "obs"), P("chan", "obs"), P("obs"), P("obs"), P())
    out_specs = (P("obs", None), P("obs", None))
    return jax.shard_map(
        per_device, mesh=mesh, in_specs=in_specs, out_specs=out_specs, check_vma=False
    )
```

profile of v0, /device:TPU:0, one launch (start us, length us, event | category | flops | bytes accessed | tf_op | source)
XLA Modules:
  0.0 699.7 jit_solution(8581663738396648842)
XLA Ops:
  8.7 2.5 fusion.5
  13.1 33.3 %all-reduce.9.cloned.1.call-done = f32[128,137,2]{0,2,1:T(2,128)} async-done(((f32[128,137,2]{0,2,1:T(2,128)}), f32[128,137,2]{0,2,1:T(2,128)}) %all-reduce.9.cloned.1.call-update) | async-done | bytes 140304 | tf_op jit(solution)/shard_map/psum | solution.py:49
  46.3 1.4 fusion.51
  48.7 5.5 all-to-all-start
  55.7 14.9 %all-reduce = s32[16]{0:T(128)S(1)} all-reduce(s32[16]{0:T(128)S(1)} %dynamic-update-slice), channel_id=1, replica_groups=mesh['obs'=8,'chan'=4] {'obs'}, use_global_device_ids=true, to_apply=%add | all-reduce | flops 16 | bytes 128
  77.3 14.5 %all_to_all.55 = bf16[8,128,137]{1,2,0:T(8,128)(2,1)} all-to-all(bf16[8,128,137]{1,2,0:T(8,128)(2,1)} %copy.105), channel_id=1, replica_groups=mesh['obs'=8,'chan'=4] {'obs'}, dimensions={0} | all-to-all | bytes 561152 | tf_op jit(solution)/shard_map/all_to_all | solution.py:92
  92.9 1.3 reshape.244
  99.4 27.9 %all-reduce.11.cloned.1.call-done = f32[128,137,2]{0,2,1:T(2,128)} async-done(((f32[128,137,2]{0,2,1:T(2,128)}), f32[128,137,2]{0,2,1:T(2,128)}) %all-reduce.11.cloned.1.call-update) | async-done | bytes 140304 | tf_op jit(solution)/shard_map/psum | solution.py:49
  127.3 1.4 fusion.49
  129.7 5.5 all-to-all-start.2
  135.3 16.2 %all-to-all-done.2 = f32[8,128,137]{1,2,0:T(8,128)S(1)} async-done(((f32[8,128,137]{1,2,0:T(8,128)}), f32[8,128,137]{1,2,0:T(8,128)S(1)}, u32[]{:S(2)}, u32[]{:S(2)}) %all-to-all-start.2) | async-done | bytes 561184 | tf_op jit(solution)/shard_map/all_to_all | solution.py:53
  151.5 1.3 copy.109
  152.8 1.7 reshape.247
  154.5 2.2 dot_general.194
  156.7 1.6 copy.110
  159.8 20.1 %all-reduce.1 = (f32[]{:T(128)}, f32[]{:T(128)}) all-reduce(f32[]{:T(128)} %get-tuple-element.10, f32[]{:T(128)} %get-tuple-element.12), channel_id=1, replica_groups=mesh['obs'=8,'chan'=4] {'obs'}, use_global_device_ids=true, to_apply=%region_3.4 | all-reduce | flops 2 | bytes 16 | tf_op jit(solution)/shard_map/psum | solution.py:81
  181.9 17.7 %psum.116 = f32[]{:T(128)} all-reduce(f32[]{:T(128)} %multiply_reduce_fusion.7), channel_id=1, replica_groups=mesh['obs'=8,'chan'=4] {'obs'}, use_global_device_ids=true, to_apply=%region_8.9 | all-reduce | flops 1 | bytes 8 | tf_op jit(solution)/shard_map/psum | solution.py:81
  202.9 2.3 reshape.249
  206.1 13.2 %all_to_all.56 = bf16[8,128,137]{1,2,0:T(8,128)(2,1)} all-to-all(bf16[8,128,137]{1,2,0:T(8,128)(2,1)} %copy.119), channel_id=1, replica_groups=mesh['obs'=8,'chan'=4] {'obs'}, dimensions={0} | all-to-all | bytes 561152 | tf_op jit(solution)/shard_map/all_to_all | solution.py:92
  220.5 1.3 reshape.250
  227.0 27.8 %all-reduce.13.cloned.1.call-done = f32[128,137,2]{0,2,1:T(2,128)} async-done(((f32[128,137,2]{0,2,1:T(2,128)}), f32[128,137,2]{0,2,1:T(2,128)}) %all-reduce.13.cloned.1.call-update) | async-done | bytes 140304 | tf_op jit(solution)/shard_map/psum | solution.py:49
  254.8 1.4 fusion.47
  256.4 22.2 %all_to_all.57 = f32[8,128,137]{1,2,0:T(8,128)S(1)} all-to-all(f32[8,128,137]{1,2,0:T(8,128)S(1)} %copy.122), channel_id=1, replica_groups=mesh['obs'=8,'chan'=4] {'obs'}, dimensions={0} | all-to-all | bytes 1122304 | tf_op jit(solution)/shard_map/all_to_all | solution.py:53
  278.6 1.3 copy.123
  279.9 1.7 reshape.253
  281.6 2.2 dot_general.206
  283.8 1.6 copy.124
  286.9 19.5 %psum.118 = f32[]{:T(128)} all-reduce(f32[]{:T(128)} %get-tuple-element.14), channel_id=1, replica_groups=mesh['obs'=8,'chan'=4] {'obs'}, use_global_device_ids=true, to_apply=%region_11.12 | all-reduce | flops 1 | bytes 8 | tf_op jit(solution)/shard_map/psum | solution.py:108
  308.3 18.1 %psum.119 = f32[]{:T(128)} all-reduce(f32[]{:T(128)} %get-tuple-element.8), channel_id=1, replica_groups=mesh['obs'=8,'chan'=4] {'obs'}, use_global_device_ids=true, to_apply=%region_13.14 | all-reduce | flops 1 | bytes 8 | tf_op jit(solution)/shard_map/psum | solution.py:81
  329.7 2.3 reshape.255
  332.9 13.0 %all_to_all.58 = bf16[8,128,137]{1,2,0:T(8,128)(2,1)} all-to-all(bf16[8,128,137]{1,2,0:T(8,128)(2,1)} %copy.128), channel_id=1, replica_groups=mesh['obs'=8,'chan'=4] {'obs'}, dimensions={0} | all-to-all | bytes 561152 | tf_op jit(solution)/shard_map/all_to_all | solution.py:92
  347.0 1.3 reshape.256
  353.5 27.8 %all-reduce.15.cloned.1.call-done = f32[128,137,2]{0,2,1:T(2,128)} async-done(((f32[128,137,2]{0,2,1:T(2,128)}), f32[128,137,2]{0,2,1:T(2,128)}) %all-reduce.15.cloned.1.call-update) | async-done | bytes 140304 | tf_op jit(solution)/shard_map/psum | solution.py:49
  381.3 1.4 fusion.45
  382.8 22.2 %all_to_all.59 = f32[8,128,137]{1,2,0:T(8,128)S(1)} all-to-all(f32[8,128,137]{1,2,0:T(8,128)S(1)} %copy.131), channel_id=1, replica_groups=mesh['obs'=8,'chan'=4] {'obs'}, dimensions={0} | all-to-all | bytes 1122304 | tf_op jit(solution)/shard_map/all_to_all | solution.py:53
  405.1 1.3 copy.132
  406.4 1.7 reshape.259
  408.1 2.2 dot_general.218
  410.3 1.6 copy.133
  413.4 19.5 %psum.121 = f32[]{:T(128)} all-reduce(f32[]{:T(128)} %get-tuple-element.16), channel_id=1, replica_groups=mesh['obs'=8,'chan'=4] {'obs'}, use_global_device_ids=true, to_apply=%region_16.17 | all-reduce | flops 1 | bytes 8 | tf_op jit(solution)/shard_map/psum | solution.py:108
  434.9 18.1 %psum.122 = f32[]{:T(128)} all-reduce(f32[]{:T(128)} %get-tuple-element.6), channel_id=1, replica_groups=mesh['obs'=8,'chan'=4] {'obs'}, use_global_device_ids=true, to_apply=%region_18.19 | all-reduce | flops 1 | bytes 8 | tf_op jit(solution)/shard_map/psum | solution.py:81
  456.3 2.3 reshape.261
  459.5 13.1 %all_to_all.60 = bf16[8,128,137]{1,2,0:T(8,128)(2,1)} all-to-all(bf16[8,128,137]{1,2,0:T(8,128)(2,1)} %copy.137), channel_id=1, replica_groups=mesh['obs'=8,'chan'=4] {'obs'}, dimensions={0} | all-to-all | bytes 561152 | tf_op jit(solution)/shard_map/all_to_all | solution.py:92
  473.7 1.3 reshape.262
  480.2 27.8 %all-reduce.17.cloned.1.call-done = f32[128,137,2]{0,2,1:T(2,128)} async-done(((f32[128,137,2]{0,2,1:T(2,128)}), f32[128,137,2]{0,2,1:T(2,128)}) %all-reduce.17.cloned.1.call-update) | async-done | bytes 140304 | tf_op jit(solution)/shard_map/psum | solution.py:49
  508.0 1.4 fusion.43
  509.6 22.3 %all_to_all.61 = f32[8,128,137]{1,2,0:T(8,128)} all-to-all(f32[8,128,137]{1,2,0:T(8,128)S(1)} %copy.140), channel_id=1, replica_groups=mesh['obs'=8,'chan'=4] {'obs'}, dimensions={0} | all-to-all | bytes 1122304 | tf_op jit(solution)/shard_map/all_to_all | solution.py:53
  531.9 2.4 copy.141
  534.3 1.7 reshape.265
  536.0 2.2 dot_general.230
  538.2 1.6 copy.142
  541.3 19.5 %psum.124 = f32[]{:T(128)} all-reduce(f32[]{:T(128)} %get-tuple-element.18), channel_id=1, replica_groups=mesh['obs'=8,'chan'=4] {'obs'}, use_global_device_ids=true, to_apply=%region_21.22 | all-reduce | flops 1 | bytes 8 | tf_op jit(solution)/shard_map/psum | solution.py:108
  562.1 1.6 multiply_reduce_fusion.1
  563.6 18.0 %psum.125 = f32[]{:T(128)} all-reduce(f32[]{:T(128)} %get-tuple-element.4), channel_id=1, replica_groups=mesh['obs'=8,'chan'=4] {'obs'}, use_global_device_ids=true, to_apply=%region_23.24 | all-reduce | flops 1 | bytes 8 | tf_op jit(solution)/shard_map/psum | solution.py:81
  585.8 2.0 reshape.267
  587.8 2.0 copy.146
  589.8 13.1 %all_to_all.62 = bf16[8,128,137]{1,2,0:T(8,128)(2,1)} all-to-all(bf16[8,128,137]{1,2,0:T(8,128)(2,1)} %copy.146), channel_id=1, replica_groups=mesh['obs'=8,'chan'=4] {'obs'}, dimensions={0} | all-to-all | bytes 561152 | tf_op jit(solution)/shard_map/all_to_all | solution.py:92
  602.9 2.0 copy.147
  604.8 2.4 reshape.268
  607.3 1.2 convolution_convert_fusion.5
  613.9 27.8 %all-reduce.19.cloned.1.call-done = f32[128,137,2]{0,2,1:T(2,128)} async-done(((f32[128,137,2]{0,2,1:T(2,128)}), f32[128,137,2]{0,2,1:T(2,128)}) %all-reduce.19.cloned.1.call-update) | async-done | bytes 140304 | tf_op jit(solution)/shard_map/psum | solution.py:49
  641.8 1.4 fusion.41
  643.3 22.2 %all_to_all.63 = f32[8,128,137]{1,2,0:T(8,128)S(1)} all-to-all(f32[8,128,137]{1,2,0:T(8,128)S(1)} %copy.149), channel_id=1, replica_groups=mesh['obs'=8,'chan'=4] {'obs'}, dimensions={0} | all-to-all | bytes 1122304 | tf_op jit(solution)/shard_map/all_to_all | solution.py:53
  669.4 19.5 %psum.127 = f32[]{:T(128)} all-reduce(f32[]{:T(128)} %get-tuple-element.20), channel_id=1, replica_groups=mesh['obs'=8,'chan'=4] {'obs'}, use_global_device_ids=true, to_apply=%region_26.27 | all-reduce | flops 1 | bytes 8 | tf_op jit(solution)/shard_map/psum | solution.py:108
  (191 shorter events, 68.0 us)
Async XLA Ops:
  7.2 65.6 %copy-start = (f32[137,137]{1,0:T(8,128)S(1)}, f32[137,137]{1,0:T(8,128)}, u32[]{:S(2)}) copy-start(f32[137,137]{1,0:T(8,128)} %param.11) | copy-start | bytes 225232
  7.2 5.8 copy-start.19
  7.2 39.1 %all-reduce.9.cloned.1.call-start = ((), (), s32[]{:S(2)}) async-start(), calls=%async_computation.11 | async-start | bytes 280576 | tf_op jit(solution)/shard_map/psum | solution.py:49
  7.9 88.8 %copy-start.14 = (f32[256]{0:T(256)}, f32[256]{0:T(256)S(1)}, u32[]{:S(2)}) copy-start(f32[256]{0:T(256)S(1)} %compare_convert_fusion.1) | copy-start | bytes 3076
  11.4 42.9 %copy-start.20 = (u32[32]{0:T(128)S(1)}, u32[32]{0:T(128)}, u32[]{:S(2)}) copy-start(u32[32]{0:T(128)} %constant.47) | copy-start | bytes 388
  13.0 114.3 %copy-start.8 = (s32[2]{0:T(128)}, s32[2]{0:T(128)S(1)}, u32[]{:S(2)}) copy-start(s32[2]{0:T(128)S(1)} %and_select_fusion) | copy-start | bytes 28
  48.7 22.3 %all-to-all-start = ((f32[8,128,137]{1,2,0:T(8,128)}), f32[8,128,137]{1,2,0:T(8,128)S(1)}, u32[]{:S(2)}, u32[]{:S(2)}) async-start(f32[8,128,137]{1,2,0:T(8,128)} %copy.102), calls=%async_computation | async-start | bytes 1179648 | tf_op jit(solution)/shard_map/all_to_all | solution.py:53
  54.2 73.1 %all-reduce.11.cloned.1.call-start = ((), (), s32[]{:S(2)}) async-start(), calls=%async_computation.12 | async-start | bytes 280576 | tf_op jit(solution)/shard_map/psum | solution.py:49
  71.0 0.9 copy-start.11
  71.0 3.8 copy-start.17
  75.1 20.9 %copy-start.1 = (bf16[256,32,137]{0,1,2:T(8,128)(2,1)S(1)}, bf16[256,32,137]{0,1,2:T(8,128)(2,1)}, u32[]{:S(2)}) copy-start(bf16[256,32,137]{0,1,2:T(8,128)(2,1)} %param.6) | copy-start | bytes 6733828
  91.8 5.0 copy-start.5
  129.7 21.8 %all-to-all-start.2 = ((f32[8,128,137]{1,2,0:T(8,128)}), f32[8,128,137]{1,2,0:T(8,128)S(1)}, u32[]{:S(2)}, u32[]{:S(2)}) async-start(f32[8,128,137]{1,2,0:T(8,128)} %copy.108), calls=%async_computation.2 | async-start | bytes 1179648 | tf_op jit(solution)/shard_map/all_to_all | solution.py:53
  135.2 119.6 %all-reduce.13.cloned.1.call-start = ((), (), s32[]{:S(2)}) async-start(), calls=%async_computation.13 | async-start | bytes 280576 | tf_op jit(solution)/shard_map/psum | solution.py:49
  152.8 5.5 copy-start.12
  156.7 45.2 %copy-start.18 = (bf16[2,8]{1,0:T(2,128)(2,1)S(1)}, bf16[2,8]{1,0:T(2,128)(2,1)}, u32[]{:S(2)}) copy-start(bf16[2,8]{1,0:T(2,128)(2,1)} %copy-done.17) | copy-start | bytes 100
  201.5 20.3 %copy-start.9 = (s32[2]{0:T(128)S(1)}, s32[2]{0:T(128)}, u32[]{:S(2)}) copy-start(s32[2]{0:T(128)} %copy-done.8) | copy-start | bytes 28
  219.3 4.9 copy-start.15
  227.0 154.3 %all-reduce.15.cloned.1.call-start = ((), (), s32[]{:S(2)}) async-start(), calls=%async_computation.14 | async-start | bytes 280576 | tf_op jit(solution)/shard_map/psum | solution.py:49
  308.3 20.4 %copy-start.3 = (f32[2,128,137]{1,2,0:T(8,128)}, f32[2,128,137]{1,2,0:T(8,128)S(1)}, u32[]{:S(2)}) copy-start(f32[2,128,137]{1,2,0:T(8,128)S(1)} %get-tuple-element.9) | copy-start | bytes 420868
  353.5 154.6 %all-reduce.17.cloned.1.call-start = ((), (), s32[]{:S(2)}) async-start(), calls=%async_computation.15 | async-start | bytes 280576 | tf_op jit(solution)/shard_map/psum | solution.py:49
  408.1 26.1 %copy-start.4 = (f32[2,128,137]{1,2,0:T(8,128)S(1)}, f32[2,128,137]{1,2,0:T(8,128)}, u32[]{:S(2)}) copy-start(f32[2,128,137]{1,2,0:T(8,128)} %copy-done.3) | copy-start | bytes 420868
  434.9 20.4 %copy-start.2 = (f32[2,128,137]{1,2,0:T(8,128)}, f32[2,128,137]{1,2,0:T(8,128)S(1)}, u32[]{:S(2)}) copy-start(f32[2,128,137]{1,2,0:T(8,128)S(1)} %get-tuple-element.7) | copy-start | bytes 420868
  472.6 4.9 copy-start.6
  480.2 161.6 %all-reduce.19.cloned.1.call-start = ((), (), s32[]{:S(2)}) async-start(), calls=%async_computation.16 | async-start | bytes 280576 | tf_op jit(solution)/shard_map/psum | solution.py:49
  602.9 8.4 %copy-start.7 = (f32[32,256]{1,0:T(8,128)S(1)}, f32[32,256]{1,0:T(8,128)}, u32[]{:S(2)}) copy-start(f32[32,256]{1,0:T(8,128)} %param.8) | copy-start | bytes 98308
  602.9 8.4 %copy-start.16 = (f32[256]{0:T(256)S(1)}, f32[256]{0:T(256)}, u32[]{:S(2)}) copy-start(f32[256]{0:T(256)} %copy-done.14) | copy-start | bytes 3076
  611.2 30.5 %copy-start.10 = (s32[2]{0:T(128)S(1)}, s32[2]{0:T(128)}, u32[]{:S(2)}) copy-start(s32[2]{0:T(128)} %copy-done.8) | copy-start | bytes 28
  665.9 2.1 copy-start.13
Sparse Core Ops, SparseCore 0:
  13.1 33.1 all-reduce.8
  99.5 27.7 all-reduce.10
  227.1 27.6 all-reduce.12
  353.6 27.6 all-reduce.14
  480.3 27.6 all-reduce.16
  614.0 27.6 all-reduce.18
where the time goes:
time: 708 us; the launch traced here: 700 us
  blocking collectives  341 us (48%)
  waiting for transfers between devices  189 us (27%)
  local copies, waits for them, and re-layouts  83.4 us (12%)
  matrix products  31.8 us (4%)
  between operations  28.7 us (4%)
  other arithmetic  15.2 us (2%)
  starting transfers between devices  11.3 us (2%)
    psum x6, waiting for transfers between devices, to_owners(): blocked = lax.psum(blocked, 'chan')  172 us
    psum x5, blocking collectives, squared(): return lax.psum(partial_sum, 'obs')  92.1 us
    all_to_all x4, blocking collectives, to_owners(): lax.all_to_all(outgoing.reshape(obs_count, share_cols, layers), 'obs', sp...  89 us
    psum x4, blocking collectives, per_device(): step_length = norm_now / lax.psum(curvature_partial_sum, 'obs')  77.8 us
    all_to_all x5, blocking collectives, per_device(): lax.all_to_all(to_outgoing.reshape(obs_count, share_cols, layers), 'obs',...  66.9 us
    dot_general x10, local copies, waits for them, and re-layouts, to_owners(): jnp.dot(take_pick, incoming.reshape(obs_count, -1), precision=lax.Precisi...  16.5 us
    all_to_all x2, waiting for transfers between devices, to_owners(): lax.all_to_all(outgoing.reshape(obs_count, share_cols, layers), 'obs', sp...  16.2 us
    reshape x10, local copies, waits for them, and re-layouts, per_device(): to_outgoing.reshape(obs_count, share_cols, layers)  15.7 us
  transfers between devices with their start and end apart: 8, of which 7 were waited for; matrix products, arithmetic and copies ran while one was open for 0% of the time, Pallas kernels for 0%

commit v1 on v0

--- a/solution.py
+++ b/solution.py
@@ -46,7 +46,8 @@
 
     def to_owners(terms):
         blocked = terms.reshape(block_count, BLOCK, layers)
-        blocked = lax.psum(blocked, "chan")
+        newest = lax.all_gather(blocked, axis_name="chan")
+        blocked = jnp.sum(newest, axis=0)
         outgoing = jnp.dot(
             send_pick, blocked.reshape(block_count, -1), precision=lax.Precision.HIGHEST
         )

time: 708 us -> 557 us (0.79)
  waiting for transfers between devices: 189 us -> 16.6 us
  blocking collectives: 341 us -> 375 us
  between operations: 28.7 us -> 15.6 us
    psum x6 -> x0, waiting for transfers between devices: 172 us -> none  [to_owners(): blocked = lax.psum(blocked, 'chan')]
    all_gather x0 -> x6, blocking collectives: none -> 45 us  [to_owners(): newest = lax.all_gather(blocked, axis_name='chan')]
    all_to_all x4, blocking collectives: 89 us -> 79.5 us  [to_owners(): lax.all_to_all(outgoing.reshape(obs_count, share_cols, layers), 'obs', sp...]
    unnamed x12 -> x6, other arithmetic: 7.93 us -> 0.83 us
    dot_general x0 -> x6, other arithmetic: none -> 7.1 us  [block_terms(): lax.dot_general(jac_part, scaled, (((1,), (1,)), ((0,), (0,))), preferred...]
  transfers between devices with their start and end apart: 8 -> 2, of which waited for: 7 -> 1; matrix products, arithmetic and copies ran while one was open for 0% -> 0% of each run, Pallas kernels for 0% -> 0%
where the time goes in v1:
time: 557 us; the launch traced here: 547 us
  blocking collectives  375 us (67%)
  local copies, waits for them, and re-layouts  83.8 us (15%)
  matrix products  27.3 us (5%)
  other arithmetic  18.8 us (3%)
  waiting for transfers between devices  16.6 us (3%)
  between operations  15.6 us (3%)
  starting transfers between devices  9.37 us (2%)
    psum x5, blocking collectives, squared(): return lax.psum(partial_sum, 'obs')  92.1 us
    all_to_all x4, blocking collectives, to_owners(): lax.all_to_all(outgoing.reshape(obs_count, share_cols, layers), 'obs', sp...  79.5 us
    psum x4, blocking collectives, per_device(): step_length = norm_now / lax.psum(curvature_partial_sum, 'obs')  77.8 us
    all_to_all x5, blocking collectives, per_device(): lax.all_to_all(to_outgoing.reshape(obs_count, share_cols, layers), 'obs',...  65.6 us
    all_gather x6, blocking collectives, to_owners(): newest = lax.all_gather(blocked, axis_name='chan')  45 us
    all_to_all x2, waiting for transfers between devices, to_owners(): lax.all_to_all(outgoing.reshape(obs_count, share_cols, layers), 'obs', sp...  16.6 us
    dot_general x10, local copies, waits for them, and re-layouts, to_owners(): jnp.dot(take_pick, incoming.reshape(obs_count, -1), precision=lax.Precisi...  16.5 us
    reshape x10, local copies, waits for them, and re-layouts, per_device(): to_outgoing.reshape(obs_count, share_cols, layers)  15.7 us
  transfers between devices with their start and end apart: 2, of which 1 were waited for; matrix products, arithmetic and copies ran while one was open for 0% of the time, Pallas kernels for 0%

profile of v1, /device:TPU:0, one launch (start us, length us, event | category | flops | bytes accessed | tf_op | source)
XLA Modules:
  0.0 546.5 jit_solution(2209927683074864746)
XLA Ops:
  2.8 2.5 fusion.5
  5.4 8.8 %all_gather.22 = f32[4,2,128,137]{2,1,3,0:T(2,128)S(1)} all-gather(f32[1,2,128,137]{2,1,3,0:T(2,128)S(1)} %all_gather_reshape.18), channel_id=1, replica_groups=mesh['obs'=8,'chan'=4] {'chan'}, dimensions={0}, use_global_device_ids=true | all-gather | bytes 701440 | tf_op jit(solution)/shard_map/all_gather | solution.py:49
  17.1 5.8 %all-to-all-start = ((f32[8,128,137]{1,2,0:T(8,128)}), f32[8,128,137]{1,2,0:T(8,128)S(1)}, u32[]{:S(2)}, u32[]{:S(2)}) async-start(f32[8,128,137]{1,2,0:T(8,128)} %copy.163), calls=%async_computation | async-start | bytes 1179648 | tf_op jit(solution)/shard_map/all_to_all | solution.py:54
  24.4 15.1 %all-reduce = s32[16]{0:T(128)S(1)} all-reduce(s32[16]{0:T(128)S(1)} %dynamic-update-slice), channel_id=1, replica_groups=mesh['obs'=8,'chan'=4] {'obs'}, use_global_device_ids=true, to_apply=%add | all-reduce | flops 16 | bytes 128
  44.0 1.2 reshape.224
  46.1 14.3 %all_to_all.55 = bf16[8,128,137]{1,2,0:T(8,128)(2,1)} all-to-all(bf16[8,128,137]{1,2,0:T(8,128)(2,1)} %copy.166), channel_id=1, replica_groups=mesh['obs'=8,'chan'=4] {'obs'}, dimensions={0} | all-to-all | bytes 561152 | tf_op jit(solution)/shard_map/all_to_all | solution.py:93
  61.6 1.3 reshape.225
  62.9 1.2 convolution_convert_fusion.9
  66.4 7.2 %all_gather.23 = f32[4,2,128,137]{2,1,3,0:T(2,128)S(1)} all-gather(f32[1,2,128,137]{2,1,3,0:T(2,128)S(1)} %all_gather_reshape.19), channel_id=1, replica_groups=mesh['obs'=8,'chan'=4] {'chan'}, dimensions={0}, use_global_device_ids=true | all-gather | bytes 701440 | tf_op jit(solution)/shard_map/all_gather | solution.py:49
  76.4 3.5 all-to-all-start.2
  80.0 16.6 %all-to-all-done.2 = f32[8,128,137]{1,2,0:T(8,128)S(1)} async-done(((f32[8,128,137]{1,2,0:T(8,128)}), f32[8,128,137]{1,2,0:T(8,128)S(1)}, u32[]{:S(2)}, u32[]{:S(2)}) %all-to-all-start.2) | async-done | bytes 561184 | tf_op jit(solution)/shard_map/all_to_all | solution.py:54
  96.6 1.3 copy.171
  97.9 1.7 reshape.227
  99.6 2.2 dot_general.194
  101.8 1.6 copy.172
  104.9 20.1 %all-reduce.1 = (f32[]{:T(128)}, f32[]{:T(128)}) all-reduce(f32[]{:T(128)} %get-tuple-element.10, f32[]{:T(128)} %get-tuple-element.12), channel_id=1, replica_groups=mesh['obs'=8,'chan'=4] {'obs'}, use_global_device_ids=true, to_apply=%region_3.4 | all-reduce | flops 2 | bytes 16 | tf_op jit(solution)/shard_map/psum | solution.py:82
  126.9 17.7 %psum.72 = f32[]{:T(128)} all-reduce(f32[]{:T(128)} %multiply_reduce_fusion.7), channel_id=1, replica_groups=mesh['obs'=8,'chan'=4] {'obs'}, use_global_device_ids=true, to_apply=%region_8.9 | all-reduce | flops 1 | bytes 8 | tf_op jit(solution)/shard_map/psum | solution.py:82
  148.1 2.3 reshape.229
  151.2 12.8 %all_to_all.56 = bf16[8,128,137]{1,2,0:T(8,128)(2,1)} all-to-all(bf16[8,128,137]{1,2,0:T(8,128)(2,1)} %copy.181), channel_id=1, replica_groups=mesh['obs'=8,'chan'=4] {'obs'}, dimensions={0} | all-to-all | bytes 561152 | tf_op jit(solution)/shard_map/all_to_all | solution.py:93
  165.2 1.4 reshape.230
  166.6 1.2 convolution_convert_fusion.8
  170.7 7.4 %all_gather.24 = f32[4,2,128,137]{2,1,3,0:T(2,128)S(1)} all-gather(f32[1,2,128,137]{2,1,3,0:T(2,128)} %all_gather_reshape.20), channel_id=1, replica_groups=mesh['obs'=8,'chan'=4] {'chan'}, dimensions={0}, use_global_device_ids=true | all-gather | bytes 701440 | tf_op jit(solution)/shard_map/all_gather | solution.py:49
  181.7 1.4 fusion.47
  183.2 19.7 %all_to_all.57 = f32[8,128,137]{1,2,0:T(8,128)S(1)} all-to-all(f32[8,128,137]{1,2,0:T(8,128)S(1)} %copy.185), channel_id=1, replica_groups=mesh['obs'=8,'chan'=4] {'obs'}, dimensions={0} | all-to-all | bytes 1122304 | tf_op jit(solution)/shard_map/all_to_all | solution.py:54
  202.9 1.3 copy.186
  204.3 1.7 reshape.232
  206.0 2.2 dot_general.206
  208.1 1.6 copy.187
  211.2 19.4 %psum.73 = f32[]{:T(128)} all-reduce(f32[]{:T(128)} %get-tuple-element.14), channel_id=1, replica_groups=mesh['obs'=8,'chan'=4] {'obs'}, use_global_device_ids=true, to_apply=%region_11.12 | all-reduce | flops 1 | bytes 8 | tf_op jit(solution)/shard_map/psum | solution.py:109
  232.7 18.1 %psum.74 = f32[]{:T(128)} all-reduce(f32[]{:T(128)} %get-tuple-element.8), channel_id=1, replica_groups=mesh['obs'=8,'chan'=4] {'obs'}, use_global_device_ids=true, to_apply=%region_13.14 | all-reduce | flops 1 | bytes 8 | tf_op jit(solution)/shard_map/psum | solution.py:82
  254.2 2.3 reshape.234
  257.4 12.8 %all_to_all.58 = bf16[8,128,137]{1,2,0:T(8,128)(2,1)} all-to-all(bf16[8,128,137]{1,2,0:T(8,128)(2,1)} %copy.191), channel_id=1, replica_groups=mesh['obs'=8,'chan'=4] {'obs'}, dimensions={0} | all-to-all | bytes 561152 | tf_op jit(solution)/shard_map/all_to_all | solution.py:93
  271.4 1.3 reshape.235
  272.7 1.2 convolution_convert_fusion.7
  276.1 7.1 %all_gather.25 = f32[4,2,128,137]{2,1,3,0:T(2,128)S(1)} all-gather(f32[1,2,128,137]{2,1,3,0:T(2,128)S(1)} %all_gather_reshape.21), channel_id=1, replica_groups=mesh['obs'=8,'chan'=4] {'chan'}, dimensions={0}, use_global_device_ids=true | all-gather | bytes 701440 | tf_op jit(solution)/shard_map/all_gather | solution.py:49
  285.3 19.7 %all_to_all.59 = f32[8,128,137]{1,2,0:T(8,128)S(1)} all-to-all(f32[8,128,137]{1,2,0:T(8,128)S(1)} %copy.195), channel_id=1, replica_groups=mesh['obs'=8,'chan'=4] {'obs'}, dimensions={0} | all-to-all | bytes 1122304 | tf_op jit(solution)/shard_map/all_to_all | solution.py:54
  305.0 1.3 copy.196
  306.4 1.7 reshape.237
  308.1 2.2 dot_general.218
  310.3 1.6 copy.197
  313.3 19.4 %psum.75 = f32[]{:T(128)} all-reduce(f32[]{:T(128)} %get-tuple-element.16), channel_id=1, replica_groups=mesh['obs'=8,'chan'=4] {'obs'}, use_global_device_ids=true, to_apply=%region_16.17 | all-reduce | flops 1 | bytes 8 | tf_op jit(solution)/shard_map/psum | solution.py:109
  334.8 18.1 %psum.76 = f32[]{:T(128)} all-reduce(f32[]{:T(128)} %get-tuple-element.6), channel_id=1, replica_groups=mesh['obs'=8,'chan'=4] {'obs'}, use_global_device_ids=true, to_apply=%region_18.19 | all-reduce | flops 1 | bytes 8 | tf_op jit(solution)/shard_map/psum | solution.py:82
  356.3 2.3 reshape.239
  359.5 12.8 %all_to_all.60 = bf16[8,128,137]{1,2,0:T(8,128)(2,1)} all-to-all(bf16[8,128,137]{1,2,0:T(8,128)(2,1)} %copy.201), channel_id=1, replica_groups=mesh['obs'=8,'chan'=4] {'obs'}, dimensions={0} | all-to-all | bytes 561152 | tf_op jit(solution)/shard_map/all_to_all | solution.py:93
  373.5 1.4 reshape.240
  374.8 1.2 convolution_convert_fusion.6
  378.9 7.2 %all_gather.26 = f32[4,2,128,137]{2,1,3,0:T(2,128)S(1)} all-gather(f32[1,2,128,137]{2,1,3,0:T(2,128)} %all_gather_reshape.22), channel_id=1, replica_groups=mesh['obs'=8,'chan'=4] {'chan'}, dimensions={0}, use_global_device_ids=true | all-gather | bytes 701440 | tf_op jit(solution)/shard_map/all_gather | solution.py:49
  389.7 20.4 %all_to_all.61 = f32[8,128,137]{1,2,0:T(8,128)} all-to-all(f32[8,128,137]{1,2,0:T(8,128)S(1)} %copy.205), channel_id=1, replica_groups=mesh['obs'=8,'chan'=4] {'obs'}, dimensions={0} | all-to-all | bytes 1122304 | tf_op jit(solution)/shard_map/all_to_all | solution.py:54
  410.2 2.4 copy.206
  412.6 1.7 reshape.242
  414.3 2.2 dot_general.230
  416.4 1.6 copy.207
  419.5 19.4 %psum.77 = f32[]{:T(128)} all-reduce(f32[]{:T(128)} %get-tuple-element.18), channel_id=1, replica_groups=mesh['obs'=8,'chan'=4] {'obs'}, use_global_device_ids=true, to_apply=%region_21.22 | all-reduce | flops 1 | bytes 8 | tf_op jit(solution)/shard_map/psum | solution.py:109
  440.3 1.6 multiply_reduce_fusion.1
  441.9 18.0 %psum.78 = f32[]{:T(128)} all-reduce(f32[]{:T(128)} %get-tuple-element.4), channel_id=1, replica_groups=mesh['obs'=8,'chan'=4] {'obs'}, use_global_device_ids=true, to_apply=%region_23.24 | all-reduce | flops 1 | bytes 8 | tf_op jit(solution)/shard_map/psum | solution.py:82
  464.0 2.0 reshape.244
  466.1 2.0 copy.211
  468.0 12.8 %all_to_all.62 = bf16[8,128,137]{1,2,0:T(8,128)(2,1)} all-to-all(bf16[8,128,137]{1,2,0:T(8,128)(2,1)} %copy.211), channel_id=1, replica_groups=mesh['obs'=8,'chan'=4] {'obs'}, dimensions={0} | all-to-all | bytes 561152 | tf_op jit(solution)/shard_map/all_to_all | solution.py:93
  480.9 2.0 copy.212
  482.8 2.4 reshape.245
  485.2 1.2 convolution_convert_fusion.5
  490.2 7.2 %all_gather.27 = f32[4,2,128,137]{2,1,3,0:T(2,128)S(1)} all-gather(f32[1,2,128,137]{2,1,3,0:T(2,128)S(1)} %all_gather_reshape.23), channel_id=1, replica_groups=mesh['obs'=8,'chan'=4] {'chan'}, dimensions={0}, use_global_device_ids=true | all-gather | bytes 701440 | tf_op jit(solution)/shard_map/all_gather | solution.py:49
  499.5 19.7 %all_to_all.63 = f32[8,128,137]{1,2,0:T(8,128)S(1)} all-to-all(f32[8,128,137]{1,2,0:T(8,128)S(1)} %copy.215), channel_id=1, replica_groups=mesh['obs'=8,'chan'=4] {'obs'}, dimensions={0} | all-to-all | bytes 1122304 | tf_op jit(solution)/shard_map/all_to_all | solution.py:54
  523.1 19.4 %psum.79 = f32[]{:T(128)} all-reduce(f32[]{:T(128)} %get-tuple-element.20), channel_id=1, replica_groups=mesh['obs'=8,'chan'=4] {'obs'}, use_global_device_ids=true, to_apply=%region_26.27 | all-reduce | flops 1 | bytes 8 | tf_op jit(solution)/shard_map/psum | solution.py:109
  (191 shorter events, 68.2 us)
Async XLA Ops:
  0.6 41.0 %copy-start = (f32[137,137]{1,0:T(8,128)S(1)}, f32[137,137]{1,0:T(8,128)}, u32[]{:S(2)}) copy-start(f32[137,137]{1,0:T(8,128)} %param.11) | copy-start | bytes 225232
  2.0 72.9 %copy-start.8 = (s32[2]{0:T(128)}, s32[2]{0:T(128)S(1)}, u32[]{:S(2)}) copy-start(s32[2]{0:T(128)S(1)} %and_select_fusion) | copy-start | bytes 28
  2.0 63.3 %copy-start.14 = (f32[256]{0:T(256)}, f32[256]{0:T(256)S(1)}, u32[]{:S(2)}) copy-start(f32[256]{0:T(256)S(1)} %compare_convert_fusion.1) | copy-start | bytes 3076
  14.5 8.4 %copy-start.20 = (u32[32]{0:T(128)S(1)}, u32[32]{0:T(128)}, u32[]{:S(2)}) copy-start(u32[32]{0:T(128)} %constant.47) | copy-start | bytes 388
  14.6 9.6 %copy-start.19 = (s32[2]{0:T(128)S(1)}, s32[2]{0:T(128)}, u32[]{:S(2)}) copy-start(s32[2]{0:T(128)} %param.10) | copy-start | bytes 28
  17.1 22.8 %all-to-all-start = ((f32[8,128,137]{1,2,0:T(8,128)}), f32[8,128,137]{1,2,0:T(8,128)S(1)}, u32[]{:S(2)}, u32[]{:S(2)}) async-start(f32[8,128,137]{1,2,0:T(8,128)} %copy.163), calls=%async_computation | async-start | bytes 1179648 | tf_op jit(solution)/shard_map/all_to_all | solution.py:54
  39.8 2.9 copy-start.11
  39.9 3.8 copy-start.17
  44.0 20.7 %copy-start.1 = (bf16[256,32,137]{0,1,2:T(8,128)(2,1)S(1)}, bf16[256,32,137]{0,1,2:T(8,128)(2,1)}, u32[]{:S(2)}) copy-start(bf16[256,32,137]{0,1,2:T(8,128)(2,1)} %param.6) | copy-start | bytes 6733828
  60.4 4.9 copy-start.5
  76.4 20.2 %all-to-all-start.2 = ((f32[8,128,137]{1,2,0:T(8,128)}), f32[8,128,137]{1,2,0:T(8,128)S(1)}, u32[]{:S(2)}, u32[]{:S(2)}) async-start(f32[8,128,137]{1,2,0:T(8,128)} %copy.170), calls=%async_computation.2 | async-start | bytes 1179648 | tf_op jit(solution)/shard_map/all_to_all | solution.py:54
  97.9 5.5 %copy-start.12 = (f32[2,8]{1,0:T(2,128)S(1)}, f32[2,8]{1,0:T(2,128)}, u32[]{:S(2)}) copy-start(f32[2,8]{1,0:T(2,128)} %copy-done.11) | copy-start | bytes 196
  101.8 45.3 %copy-start.18 = (bf16[2,8]{1,0:T(2,128)(2,1)S(1)}, bf16[2,8]{1,0:T(2,128)(2,1)}, u32[]{:S(2)}) copy-start(bf16[2,8]{1,0:T(2,128)(2,1)} %copy-done.17) | copy-start | bytes 100
  146.7 19.9 %copy-start.9 = (s32[2]{0:T(128)S(1)}, s32[2]{0:T(128)}, u32[]{:S(2)}) copy-start(s32[2]{0:T(128)} %copy-done.8) | copy-start | bytes 28
  164.1 4.9 copy-start.15
  232.7 20.5 %copy-start.3 = (f32[2,128,137]{1,2,0:T(8,128)}, f32[2,128,137]{1,2,0:T(8,128)S(1)}, u32[]{:S(2)}) copy-start(f32[2,128,137]{1,2,0:T(8,128)S(1)} %get-tuple-element.9) | copy-start | bytes 420868
  308.1 26.1 %copy-start.4 = (f32[2,128,137]{1,2,0:T(8,128)S(1)}, f32[2,128,137]{1,2,0:T(8,128)}, u32[]{:S(2)}) copy-start(f32[2,128,137]{1,2,0:T(8,128)} %copy-done.3) | copy-start | bytes 420868
  334.8 20.4 %copy-start.2 = (f32[2,128,137]{1,2,0:T(8,128)}, f32[2,128,137]{1,2,0:T(8,128)S(1)}, u32[]{:S(2)}) copy-start(f32[2,128,137]{1,2,0:T(8,128)S(1)} %get-tuple-element.7) | copy-start | bytes 420868
  372.3 4.9 copy-start.6
  480.9 8.3 %copy-start.7 = (f32[32,256]{1,0:T(8,128)S(1)}, f32[32,256]{1,0:T(8,128)}, u32[]{:S(2)}) copy-start(f32[32,256]{1,0:T(8,128)} %param.8) | copy-start | bytes 98308
  480.9 8.3 %copy-start.16 = (f32[256]{0:T(256)S(1)}, f32[256]{0:T(256)}, u32[]{:S(2)}) copy-start(f32[256]{0:T(256)} %copy-done.14) | copy-start | bytes 3076
  490.2 8.7 %copy-start.10 = (s32[2]{0:T(128)S(1)}, s32[2]{0:T(128)}, u32[]{:S(2)}) copy-start(s32[2]{0:T(128)} %copy-done.8) | copy-start | bytes 28
  519.5 2.1 copy-start.13
